TPU v7x, 512 devices: a whole 4x8x8 slice. The times are simulated.
512 devices in a mesh: trial: 4 (over x), span: 16 (over y, core), heads: 8 (over z).
Axes of the slice: x: 4, y: 8, z: 8, core: 2. Of those that a mesh axis runs over, the one named last changes fastest.
Arguments:
- latents: bfloat16 [64, 4096, 512], P('trial', ('span', 'heads')), parts along dimension 0, may hold values from -6 to 6
- rotary_rows: bfloat16 [64, 4096, 64], P('trial', ('span', 'heads')), parts along dimension 0, may hold values from -6 to 6
- latent_gain: float32 [512], replicated, may hold values from 0.25 to 1.75
- key_up: bfloat16 [2048, 16, 128], P('trial', 'heads'), parts along dimension 0, may hold values from -0.25 to 0.25
- value_up: bfloat16 [2048, 16, 128], P('trial', 'heads'), parts along dimension 0, may hold values from -0.25 to 0.25
Outputs:
- cache_keys: bfloat16 [64, 16, 192, 4096], P(('trial', 'span'), 'heads'), parts along dimension 0
- cache_values: bfloat16 [64, 4096, 16, 128], P(('trial', 'span'), None, 'heads'), parts along dimension 0
There are 4 independent parts, one for each index of `trial`. A program takes and returns all parts, laid end to end along the dimension named above; an argument that names none is the same for every part. Nothing has to cross between parts.
All inputs are finite; a program needn't handle non-finite values.
Results may differ from a plain program's by a relative error of at most 0.0049.
Values may be sent and summed in bfloat16 or wider, within the bound.
No kernel may reach another device: no remote copies, remote signals or barrier semaphores. Data moves between devices by JAX's collectives and lax.ppermute only.
A program may use at most 64 MiB of HBM per device.

v0:
```python
import jax
import jax.numpy as jnp
from jax import lax
from jax.sharding import PartitionSpec as P


def in_one_piece(arrays, axis, split_dim, concat_dim, along):
    ends, at = ([], 0)
    for a in arrays[:-1]:
        at += a.shape[along]
        ends.append(at)
    both = jnp.concatenate(arrays, axis=along)
    return tuple(
        jnp.split(
            lax.all_to_all(both, axis, split_axis=split_dim, concat_axis=concat_dim, tiled=True),
            ends,
            axis=along,
        )
    )


def widen_rows(rows, rotary, key_up, value_up):
    wide_keys = jnp.einsum(
        "btr,rhk->bthk", rows, key_up, preferred_element_type=jnp.float32
    ).astype(jnp.bfloat16)
    shared = jnp.broadcast_to(rotary[:, :, None], wide_keys.shape[:3] + rotary.shape[2:])
    wide_values = jnp.einsum(
        "btr,rhk->bthk", rows, value_up, preferred_element_type=jnp.float32
    ).astype(jnp.bfloat16)
    return (jnp.concatenate([wide_keys, shared], axis=-1), wide_values)


def unit_rows(vectors, row_gain):
    return (
        vectors * lax.rsqrt(jnp.mean(vectors * vectors, axis=-1, keepdims=True) + 1e-06) * row_gain
    )


def shards(latents, rotary_rows, latent_gain, key_up, value_up):
    rows_ready = unit_rows(latents.astype(jnp.float32), latent_gain).astype(jnp.bfloat16)
    rows_moved, rotary_moved = in_one_piece((rows_ready, rotary_rows), "span", 0, 1, 2)
    rows_cut = rows_moved.reshape(
        rows_moved.shape[0], lax.axis_size("span"), -1, rows_moved.shape[2]
    )
    rotary_cut = rotary_moved.reshape(
        rotary_moved.shape[0], lax.axis_size("span"), -1, rotary_moved.shape[2]
    )
    rows_joined, rotary_joined = (
        lax.all_gather(rows_cut, "heads", axis=2, tiled=True),
        lax.all_gather(rotary_cut, "heads", axis=2, tiled=True),
    )
    rows_whole = rows_joined.reshape(rows_joined.shape[0], -1, rows_joined.shape[3])
    rotary_whole = rotary_joined.reshape(rotary_joined.shape[0], -1, rotary_joined.shape[3])
    cache_keys, cache_values = widen_rows(rows_whole, rotary_whole, key_up, value_up)
    cache_keys = jnp.transpose(cache_keys, (0, 2, 3, 1))
    return (cache_keys, cache_values)


def solution(mesh):
    return jax.shard_map(
        shards,
        mesh=mesh,
        in_specs=(
            P("trial", ("span", "heads"), None),
            P("trial", ("span", "heads"), None),
            P(),
            P("trial", "heads", None),
            P("trial", "heads", None),
        ),
        out_specs=(
            P(("trial", "span"), "heads", None, None),
            P(("trial", "span"), None, "heads", None),
        ),
        check_vma=False,
    )
```

profile of v0, /device:TPU:6, one launch (start us, length us, event | category | flops | bytes accessed | tf_op | source)
XLA Modules:
  0.0 137.5 jit_solution(17999335200704216173)
XLA Ops:
  7.2 0.0 copy-start
  7.2 0.0 copy-start.2
  7.2 0.0 all-gather.2.cloned.1.call-start
  7.2 1.3 fusion.1
  8.5 1.2 fusion.3
  9.8 1.0 pad_maximum_fusion
  10.7 27.0 %all_to_all.12 = bf16[16,32,576]{2,1,0:T(8,128)(2,1)S(1)} all-to-all(bf16[16,32,576]{2,1,0:T(8,128)(2,1)S(1)} %pad_maximum_fusion), channel_id=1, replica_groups=mesh['trial'=4,'span'=16,'heads'=8] {'span'}, dimensions={0} | all-to-all | bytes 1179648 | tf_op jit(solution)/shard_map/all_to_all | solution.py:15
  37.7 0.8 split.8
  38.5 0.0 all-gather.2.cloned.1.call-update
  38.6 0.0 copy-done.2
  38.6 0.2 copy.14
  38.8 0.1 copy.15
  38.8 36.3 %all_gather.7 = bf16[1,16,256,64]{3,1,0,2:T(8,128)(2,1)S(1)} all-gather(bf16[1,16,32,64]{3,1,0,2:T(8,128)(2,1)S(1)} %copy.15), channel_id=1, replica_groups=mesh['trial'=4,'span'=16,'heads'=8] {'heads'}, dimensions={2}, use_global_device_ids=true | all-gather | bytes 589824 | tf_op jit(solution)/shard_map/all_gather | solution.py:50
  75.1 1.3 copy.16
  76.5 0.2 copy.19
  76.7 27.0 %all-gather.2.cloned.1.call-done = bf16[1,16,256,512]{3,2,1,0:T(8,128)(2,1)} async-done(((bf16[1,16,32,512]{3,2,1,0:T(8,128)(2,1)}), bf16[1,16,256,512]{3,2,1,0:T(8,128)(2,1)}) %all-gather.2.cloned.1.call-update) | async-done | bytes 4194320 | tf_op jit(solution)/shard_map/all_gather | solution.py:49
  103.7 3.5 %fusion.5 = f32[4096,256]{0,1:S(1)} fusion(bf16[4096,512]{1,0:T(8,128)(2,1)} %bitcast.23, bf16[512,256]{0,1:T(8,128)(2,1)S(1)} %bitcast.30), kind=kOutput, calls=%fused_computation.12 | convolution fusion | flops 1073741824 | bytes 8650752
  107.1 0.0 copy-start.1
  107.1 0.3 convert_bitcast_fusion
  107.4 0.0 copy-done
  107.4 1.9 %copy-done.1 = bf16[1,16,256,512]{3,2,1,0:T(8,128)(2,1)S(1)} copy-done((bf16[1,16,256,512]{3,2,1,0:T(8,128)(2,1)S(1)}, bf16[1,16,256,512]{3,2,1,0:T(8,128)(2,1)}, u32[]{:S(2)}) %copy-start.1) | copy-done | bytes 4194328
  109.3 1.3 fusion
  110.6 18.1 %copy.18 = bf16[1,4096,2,128]{3,2,1,0:T(2,128)(2,1)} copy(bf16[1,4096,2,128]{3,1,2,0:T(8,128)(2,1)S(1)} %fusion) | data formatting | bytes 4194304
  128.7 0.1 broadcast_in_dim.10
  128.8 1.9 %maximum_bitcast_fusion = bf16[1,2,192,4096]{3,2,1,0:T(8,128)(2,1)} fusion(bf16[1,4096,2,64]{1,3,2,0:T(8,128)(2,1)S(1)} %broadcast_in_dim.10, bf16[1,4096,2,128]{1,3,2,0:T(8,128)(2,1)S(1)} %convert_bitcast_fusion), kind=kLoop, calls=%fused_computation.2 | loop fusion | flops 6291456 | bytes 6291456 | tf_op jit(solution)/shard_map/transpose | solution.py:55
  (2 shorter events, 0.0 us)
Async XLA Ops:
  7.2 100.3 %copy-start = (bf16[512,2,128]{2,1,0:T(2,128)(2,1)S(1)}, bf16[512,2,128]{2,1,0:T(2,128)(2,1)}, u32[]{:S(2)}) copy-start(bf16[512,2,128]{2,1,0:T(2,128)(2,1)} %param.9) | copy-start | bytes 786436
  7.2 31.4 %copy-start.2 = (bf16[512,2,128]{2,1,0:T(2,128)(2,1)S(1)}, bf16[512,2,128]{2,1,0:T(2,128)(2,1)}, u32[]{:S(2)}) copy-start(bf16[512,2,128]{2,1,0:T(2,128)(2,1)} %param.8) | copy-start | bytes 786436
  7.2 96.5 %all-gather.2.cloned.1.call-start = ((), (), s32[]{:S(2)}) async-start(), calls=%async_computation.1 | async-start | bytes 4718592 | tf_op jit(solution)/shard_map/all_gather | solution.py:49
  107.1 2.2 %copy-start.1 = (bf16[1,16,256,512]{3,2,1,0:T(8,128)(2,1)S(1)}, bf16[1,16,256,512]{3,2,1,0:T(8,128)(2,1)}, u32[]{:S(2)}) copy-start(bf16[1,16,256,512]{3,2,1,0:T(8,128)(2,1)} %all-gather.2.cloned.1.call-done) | copy-start | bytes 12582916
Sparse Core Ops, SparseCore 0:
  38.7 64.9 all-gather.1
where the time goes:
time: 139 us; the launch traced here: 138 us
  blocking collectives  63.3 us (46%)
  waiting for transfers between devices  27 us (19%)
  local copies, waits for them, and re-layouts  22.7 us (16%)
  between operations  14.2 us (10%)
  other arithmetic  5.63 us (4%)
  matrix products  4.72 us (3%)
    all_gather x1, blocking collectives, shards(): lax.all_gather(rotary_cut, 'heads', axis=2, tiled=True)  36.3 us
    all_gather x1, waiting for transfers between devices, shards(): lax.all_gather(rows_cut, 'heads', axis=2, tiled=True)  27 us
    all_to_all x1, blocking collectives, in_one_piece(): lax.all_to_all(both, axis, split_axis=split_dim, concat_axis=concat_dim,...  27 us
    unnamed x9, local copies, waits for them, and re-layouts  20.4 us
    unnamed x1, matrix products  3.47 us
  transfers between devices with their start and end apart: 1, of which 1 were waited for; matrix products, arithmetic and copies ran while one was open for 1% of the time, Pallas kernels for 0%

commit v1 on v0

v1 whole, which is shorter than its diff:
```python
import functools

import jax
import jax.numpy as jnp
from jax import lax
from jax.experimental import pallas as pl
from jax.experimental.pallas import tpu as pltpu
from jax.sharding import PartitionSpec as P

CHUNKS = 2


def pack_kernel(lat_ref, rot_ref, gain_ref, out_ref):
    x = lat_ref[...].astype(jnp.float32)
    scale = lax.rsqrt(jnp.mean(x * x, axis=-1, keepdims=True) + 1e-06)
    rows = (x * scale * gain_ref[...][None]).astype(jnp.bfloat16)
    n, width = x.shape[1], x.shape[2]
    for j in range(width // 128):
        out_ref[:, j * n : (j + 1) * n, :] = rows[:, :, j * 128 : (j + 1) * 128]
    base, half = (width // 128) * n, n // 2
    rot = rot_ref[...]
    out_ref[:, base : base + half, 0:64] = rot[:, :half]
    out_ref[:, base : base + half, 64:128] = rot[:, half:]


def pack(latents, rotary, gain):
    s, n, width = latents.shape
    return pl.pallas_call(
        pack_kernel,
        out_shape=jax.ShapeDtypeStruct((s, n * (width + 64) // 128, 128), jnp.bfloat16),
        name="pack",
    )(latents, rotary, gain.reshape(1, width))


def expand_kernel(z_ref, wk_ref, wv_ref, *refs, zs, n, width, first):
    x_refs = refs[:zs]
    keys_ref, vals_ref, rows_s, rot_s = refs[zs + (0 if first else 2) :]
    z = z_ref[0]
    per = zs * n
    sps = x_refs[0].shape[0]
    half = n // 2
    base = (width // 128) * n
    for s in range(sps):
        for k, x_ref in enumerate(x_refs):
            at = pl.multiple_of(s * per + lax.rem(z + zs - k, zs) * n, n)
            for j in range(width // 128):
                rows_s[pl.ds(at, n), j * 128 : (j + 1) * 128] = x_ref[s, j * n : (j + 1) * n, :]
            rot_s[pl.ds(at, half), :] = x_ref[s, base : base + half, 0:64]
            rot_s[pl.ds(at + half, half), :] = x_ref[s, base : base + half, 64:128]
    ri = lax.broadcasted_iota(jnp.int32, (256, 256), 0)
    ci = lax.broadcasted_iota(jnp.int32, (256, 256), 1)
    target = jnp.where(ci < 128, 2 * ci, 2 * ci - 255)
    weave = (ri == target).astype(jnp.bfloat16)
    for s in range(sps):
        r = rows_s[s * per : (s + 1) * per, :]
        kt = lax.dot_general(
            wk_ref[...], r, (((1,), (1,)), ((), ())), preferred_element_type=jnp.float32
        ).astype(jnp.bfloat16)
        rt = rot_s[s * per : (s + 1) * per, :].T
        for h in range(2):
            keys_ref[h, 0:128, s * per : (s + 1) * per] = kt[h * 128 : (h + 1) * 128]
            keys_ref[h, 128:192, s * per : (s + 1) * per] = rt
        v = jnp.dot(r, wv_ref[...], preferred_element_type=jnp.float32).astype(jnp.bfloat16)
        for b in range(per // 128):
            both = jnp.concatenate(
                [v[b * 128 : (b + 1) * 128, :128], v[b * 128 : (b + 1) * 128, 128:]], axis=0
            )
            m = jnp.dot(weave, both, preferred_element_type=jnp.float32).astype(jnp.bfloat16)
            at = (s * per + b * 128) * 2
            vals_ref[at : at + 256, :] = m


def expand(z, wk, wv, slots, offset, length, prev, sp_step=2):
    zs = len(slots)
    sps, packed, _ = slots[0].shape
    width = wk.shape[1]
    n = packed * 128 // (width + 64)
    per = zs * n
    steps = sps // sp_step
    off = offset // sp_step
    first = prev is None
    kshape = jax.ShapeDtypeStruct((2, 192, length), jnp.bfloat16)
    vshape = jax.ShapeDtypeStruct((2 * length, 128), jnp.bfloat16)
    in_specs = [
        pl.BlockSpec(memory_space=pltpu.SMEM),
        pl.BlockSpec(wk.shape, lambda i: (0, 0)),
        pl.BlockSpec(wv.shape, lambda i: (0, 0)),
    ] + [pl.BlockSpec((sp_step, packed, 128), lambda i: (i, 0, 0)) for _ in slots]
    args = [z, wk, wv, *slots]
    aliases = {}
    if not first:
        aliases = {len(args): 0, len(args) + 1: 1}
        in_specs += [pl.BlockSpec(memory_space=pl.ANY)] * 2
        args += list(prev)
    return pl.pallas_call(
        functools.partial(expand_kernel, zs=zs, n=n, width=width, first=first),
        grid=(steps,),
        in_specs=in_specs,
        out_specs=[
            pl.BlockSpec((2, 192, sp_step * per), lambda i: (0, 0, i + off)),
            pl.BlockSpec((sp_step * per * 2, 128), lambda i: (i + off, 0)),
        ],
        out_shape=[kshape, vshape],
        scratch_shapes=[
            pltpu.VMEM((sp_step * per, width), jnp.bfloat16),
            pltpu.VMEM((sp_step * per, 64), jnp.bfloat16),
        ],
        input_output_aliases=aliases,
        name="expand",
    )(*args)


def ring(chunks, axis):
    n = lax.axis_size(axis)
    right = [(i, (i + 1) % n) for i in range(n)]
    left = [(i, (i - 1) % n) for i in range(n)]
    slots = [[x] + [None] * (n - 1) for x in chunks]
    for step in range(1, n // 2 + 1):
        for c in range(len(chunks)):
            if step < n // 2 or c % 2 == 0:
                slots[c][step] = lax.ppermute(slots[c][step - 1], axis, right)
            if step < n // 2 or c % 2 == 1:
                slots[c][n - step] = lax.ppermute(slots[c][(n - step + 1) % n], axis, left)
    return slots


def shards(latents, rotary_rows, latent_gain, key_up, value_up):
    width = latents.shape[2]
    packed = pack(latents, rotary_rows, latent_gain)
    moved = lax.all_to_all(packed, "span", split_axis=0, concat_axis=0, tiled=True)
    spans = moved.shape[0]
    each = spans // CHUNKS
    slots = ring([moved[c * each : (c + 1) * each] for c in range(CHUNKS)], "heads")
    wk = key_up.reshape(width, -1).T
    wv = value_up.reshape(width, -1)
    z = lax.axis_index("heads").astype(jnp.int32).reshape(1)
    length = spans * lax.axis_size("heads") * latents.shape[1]
    outs = None
    for c in range(CHUNKS):
        outs = expand(z, wk, wv, slots[c], c * each, length, outs)
    keys, vals = outs
    return (keys[None], vals.reshape(1, length, 2, 128))


def solution(mesh):
    return jax.shard_map(
        shards,
        mesh=mesh,
        in_specs=(
            P("trial", ("span", "heads"), None),
            P("trial", ("span", "heads"), None),
            P(),
            P("trial", "heads", None),
            P("trial", "heads", None),
        ),
        out_specs=(
            P(("trial", "span"), "heads", None, None),
            P(("trial", "span"), None, "heads", None),
        ),
        check_vma=False,
    )
```

time: 139 us -> 103 us (0.74)
  starting transfers between devices: 0.04 us -> 51.7 us
  blocking collectives: 63.3 us -> 26.1 us
  waiting for transfers between devices: 27 us -> 4.89 us
  local copies, waits for them, and re-layouts: 22.7 us -> 3.6 us
  Pallas kernels: 0 us -> 14.5 us
  between operations: 14.2 us -> 1 us
  other arithmetic: 5.63 us -> 0 us
  matrix products: 4.72 us -> 0 us
    ppermute x0 -> x14, starting transfers between devices: none -> 51.7 us  [the longest x7 34.1 us: ring(): slots[c][n - step] = lax.ppermute(slots[c][(n - step + 1) % n], axis, left)]
    all_gather x1 -> x0, blocking collectives: 36.3 us -> none  [shards(): lax.all_gather(rotary_cut, 'heads', axis=2, tiled=True)]
    all_gather x1 -> x0, waiting for transfers between devices: 27 us -> none  [shards(): lax.all_gather(rows_cut, 'heads', axis=2, tiled=True)]
    unnamed x9 -> x26, local copies, waits for them, and re-layouts: 20.4 us -> 3.56 us
    pallas_call x0 -> x3, Pallas kernels: none -> 14.5 us  [the longest x2 12.4 us: expand(): pl.pallas_call(functools.partial(expand_kernel, zs=zs, n=n, width=width,...]
    ppermute x0 -> x14, waiting for transfers between devices: none -> 4.89 us  [the longest x7 4.87 us: ring(): slots[c][step] = lax.ppermute(slots[c][step - 1], axis, right)]
    unnamed x1 -> x0, matrix products: 3.47 us -> none
    transpose x1 -> x0, other arithmetic: 1.87 us -> none  [shards(): cache_keys = jnp.transpose(cache_keys, (0, 2, 3, 1))]
  transfers between devices with their start and end apart: 1 -> 14, of which waited for: 1 -> 2; matrix products, arithmetic and copies ran while one was open for 1% -> 3% of each run, Pallas kernels for 0% -> 6%
where the time goes in v1:
time: 103 us; the launch traced here: 102 us
  starting transfers between devices  51.7 us (50%)
  blocking collectives  26.1 us (25%)
  Pallas kernels  14.5 us (14%)
  waiting for transfers between devices  4.89 us (5%)
  local copies, waits for them, and re-layouts  3.6 us (3%)
    ppermute x7, starting transfers between devices, ring(): slots[c][n - step] = lax.ppermute(slots[c][(n - step + 1) % n], axis, left)  34.1 us
    all_to_all x1, blocking collectives, shards(): lax.all_to_all(packed, 'span', split_axis=0, concat_axis=0, tiled=True)  26.1 us
    ppermute x7, starting transfers between devices, ring(): slots[c][step] = lax.ppermute(slots[c][step - 1], axis, right)  17.6 us
    pallas_call x2, Pallas kernels, expand(): pl.pallas_call(functools.partial(expand_kernel, zs=zs, n=n, width=width,...  12.4 us
    ppermute x7, waiting for transfers between devices, ring(): slots[c][step] = lax.ppermute(slots[c][step - 1], axis, right)  4.87 us
    unnamed x26, local copies, waits for them, and re-layouts  3.56 us
    pallas_call x1, Pallas kernels, pack(): pl.pallas_call(pack_kernel, out_shape=jax.ShapeDtypeStruct((s, n * (width...  2.15 us
  transfers between devices with their start and end apart: 14, of which 2 were waited for; matrix products, arithmetic and copies ran while one was open for 3% of the time, Pallas kernels for 6%

profile of v1, /device:TPU:6, one launch (start us, length us, event | category | flops | bytes accessed | tf_op | source)
XLA Modules:
  0.0 101.8 jit_solution(4087721921911951798)
XLA Ops:
  0.6 2.1 %pack.1 = bf16[16,144,128]{2,1,0:T(8,128)(2,1)} custom-call(bf16[16,32,512]{2,1,0:T(8,128)(2,1)} %lat_ref.1, bf16[16,32,64]{2,1,0:T(8,128)(2,1)} %rot_ref.1, f32[1,512]{1,0:T(1,128)} %bitcast.18), custom_call_target="tpu_custom_call" | custom-call | tf_op jit(solution)/shard_map/pack/pallas_call | solution.py:28
  2.8 26.1 %all_to_all.5 = bf16[16,144,128]{2,1,0:T(8,128)(2,1)S(1)} all-to-all(bf16[16,144,128]{2,1,0:T(8,128)(2,1)} %pack.1), channel_id=1, replica_groups=mesh['trial'=4,'span'=16,'heads'=8] {'span'}, dimensions={0} | all-to-all | bytes 1179648 | tf_op jit(solution)/shard_map/all_to_all | solution.py:130
  29.0 0.0 copy-start.1
  29.0 0.0 copy-start
  29.0 4.3 %collective-permute-start.7 = (bf16[8,144,128]{2,1,0:T(8,128)(2,1)S(1)}, bf16[8,144,128]{2,1,0:T(8,128)(2,1)S(1)}, u32[]{:S(2)}, u32[]{:S(2)}) collective-permute-start(bf16[8,144,128]{2,1,0:T(8,128)(2,1)S(1)} %get-tuple-element.10.refs_0_), channel_id=1, source_target_pairs={{0,1},{1,2},{2,3},{3,4},{4,5},{5,6},{6,7},{7,0},{8,9},{9,10},{10,1... | collective-permute-start | bytes 884744 | tf_op jit(solution)/shard_map/ppermute | solution.py:121
  33.3 8.6 %collective-permute-start.3 = (bf16[8,144,128]{2,1,0:T(8,128)(2,1)S(1)}, bf16[8,144,128]{2,1,0:T(8,128)(2,1)S(1)}, u32[]{:S(2)}, u32[]{:S(2)}) collective-permute-start(bf16[8,144,128]{2,1,0:T(8,128)(2,1)S(1)} %get-tuple-element.11.refs_0_), channel_id=1, source_target_pairs={{0,7},{1,0},{2,1},{3,2},{4,3},{5,4},{6,5},{7,6},{8,15},{9,8},{10,9... | collective-permute-start | bytes 884744 | tf_op jit(solution)/shard_map/ppermute | solution.py:123
  41.9 3.9 %collective-permute-start.11 = (bf16[8,144,128]{2,1,0:T(8,128)(2,1)S(1)}, bf16[8,144,128]{2,1,0:T(8,128)(2,1)S(1)}, u32[]{:S(2)}, u32[]{:S(2)}) collective-permute-start(bf16[8,144,128]{2,1,0:T(8,128)(2,1)S(1)} %get-tuple-element.10.refs_0_), channel_id=1, source_target_pairs={{0,7},{1,0},{2,1},{3,2},{4,3},{5,4},{6,5},{7,6},{8,15},{9,8},{10,9... | collective-permute-start | bytes 884744 | tf_op jit(solution)/shard_map/ppermute | solution.py:123
  45.8 1.7 %collective-permute-done.7.refs_1_ = bf16[8,144,128]{2,1,0:T(8,128)(2,1)S(1)} collective-permute-done((bf16[8,144,128]{2,1,0:T(8,128)(2,1)S(1)}, bf16[8,144,128]{2,1,0:T(8,128)(2,1)S(1)}, u32[]{:S(2)}, u32[]{:S(2)}) %collective-permute-start.7) | collective-permute-done | bytes 294944 | tf_op jit(solution)/shard_map/ppermute | solution.py:121
  47.5 0.0 copy-start.3
  47.5 1.9 %collective-permute-start.8 = (bf16[8,144,128]{2,1,0:T(8,128)(2,1)S(1)}, bf16[8,144,128]{2,1,0:T(8,128)(2,1)S(1)}, u32[]{:S(2)}, u32[]{:S(2)}) collective-permute-start(bf16[8,144,128]{2,1,0:T(8,128)(2,1)S(1)} %collective-permute-done.7.refs_1_), channel_id=1, source_target_pairs={{0,1},{1,2},{2,3},{3,4},{4,5},{5,6},{6,7},{7,0},{8,9},{9,10},{10,1... | collective-permute-start | bytes 884744 | tf_op jit(solution)/shard_map/ppermute | solution.py:121
  49.4 1.9 %collective-permute-start = (bf16[8,144,128]{2,1,0:T(8,128)(2,1)S(1)}, bf16[8,144,128]{2,1,0:T(8,128)(2,1)S(1)}, u32[]{:S(2)}, u32[]{:S(2)}) collective-permute-start(bf16[8,144,128]{2,1,0:T(8,128)(2,1)S(1)} %get-tuple-element.11.refs_0_), channel_id=1, source_target_pairs={{0,1},{1,2},{2,3},{3,4},{4,5},{5,6},{6,7},{7,0},{8,9},{9,10},{10,1... | collective-permute-start | bytes 884744 | tf_op jit(solution)/shard_map/ppermute | solution.py:121
  51.3 0.0 collective-permute-done.3.refs_7_
  51.3 0.0 copy-start.2
  51.4 5.1 %collective-permute-start.4 = (bf16[8,144,128]{2,1,0:T(8,128)(2,1)S(1)}, bf16[8,144,128]{2,1,0:T(8,128)(2,1)S(1)}, u32[]{:S(2)}, u32[]{:S(2)}) collective-permute-start(bf16[8,144,128]{2,1,0:T(8,128)(2,1)S(1)} %collective-permute-done.3.refs_7_), channel_id=1, source_target_pairs={{0,7},{1,0},{2,1},{3,2},{4,3},{5,4},{6,5},{7,6},{8,15},{9,8},{10,9... | collective-permute-start | bytes 884744 | tf_op jit(solution)/shard_map/ppermute | solution.py:123
  56.5 0.0 collective-permute-done.11.refs_7_
  56.5 0.0 copy-start.6
  56.5 4.1 %collective-permute-start.12 = (bf16[8,144,128]{2,1,0:T(8,128)(2,1)S(1)}, bf16[8,144,128]{2,1,0:T(8,128)(2,1)S(1)}, u32[]{:S(2)}, u32[]{:S(2)}) collective-permute-start(bf16[8,144,128]{2,1,0:T(8,128)(2,1)S(1)} %collective-permute-done.11.refs_7_), channel_id=1, source_target_pairs={{0,7},{1,0},{2,1},{3,2},{4,3},{5,4},{6,5},{7,6},{8,15},{9,8},{10,9... | collective-permute-start | bytes 884744 | tf_op jit(solution)/shard_map/ppermute | solution.py:123
  60.6 0.0 collective-permute-done.8.refs_2_
  60.6 0.0 copy-start.7
  60.6 1.9 %collective-permute-start.9 = (bf16[8,144,128]{2,1,0:T(8,128)(2,1)S(1)}, bf16[8,144,128]{2,1,0:T(8,128)(2,1)S(1)}, u32[]{:S(2)}, u32[]{:S(2)}) collective-permute-start(bf16[8,144,128]{2,1,0:T(8,128)(2,1)S(1)} %collective-permute-done.8.refs_2_), channel_id=1, source_target_pairs={{0,1},{1,2},{2,3},{3,4},{4,5},{5,6},{6,7},{7,0},{8,9},{9,10},{10,1... | collective-permute-start | bytes 884744 | tf_op jit(solution)/shard_map/ppermute | solution.py:121
  62.5 3.2 %collective-permute-done.refs_1_ = bf16[8,144,128]{2,1,0:T(8,128)(2,1)S(1)} collective-permute-done((bf16[8,144,128]{2,1,0:T(8,128)(2,1)S(1)}, bf16[8,144,128]{2,1,0:T(8,128)(2,1)S(1)}, u32[]{:S(2)}, u32[]{:S(2)}) %collective-permute-start) | collective-permute-done | bytes 294944 | tf_op jit(solution)/shard_map/ppermute | solution.py:121
  65.7 0.0 copy-start.4
  65.7 1.9 %collective-permute-start.1 = (bf16[8,144,128]{2,1,0:T(8,128)(2,1)S(1)}, bf16[8,144,128]{2,1,0:T(8,128)(2,1)S(1)}, u32[]{:S(2)}, u32[]{:S(2)}) collective-permute-start(bf16[8,144,128]{2,1,0:T(8,128)(2,1)S(1)} %collective-permute-done.refs_1_), channel_id=1, source_target_pairs={{0,1},{1,2},{2,3},{3,4},{4,5},{5,6},{6,7},{7,0},{8,9},{9,10},{10,1... | collective-permute-start | bytes 884744 | tf_op jit(solution)/shard_map/ppermute | solution.py:121
  67.6 0.0 collective-permute-done.4.refs_6_
  67.6 0.0 copy-start.5
  67.6 5.1 %collective-permute-start.5 = (bf16[8,144,128]{2,1,0:T(8,128)(2,1)S(1)}, bf16[8,144,128]{2,1,0:T(8,128)(2,1)S(1)}, u32[]{:S(2)}, u32[]{:S(2)}) collective-permute-start(bf16[8,144,128]{2,1,0:T(8,128)(2,1)S(1)} %collective-permute-done.4.refs_6_), channel_id=1, source_target_pairs={{0,7},{1,0},{2,1},{3,2},{4,3},{5,4},{6,5},{7,6},{8,15},{9,8},{10,9... | collective-permute-start | bytes 884744 | tf_op jit(solution)/shard_map/ppermute | solution.py:123
  72.8 0.0 collective-permute-done.12.refs_6_
  72.8 0.0 copy-start.9
  72.8 2.1 %collective-permute-start.13 = (bf16[8,144,128]{2,1,0:T(8,128)(2,1)S(1)}, bf16[8,144,128]{2,1,0:T(8,128)(2,1)}, u32[]{:S(2)}, u32[]{:S(2)}) collective-permute-start(bf16[8,144,128]{2,1,0:T(8,128)(2,1)S(1)} %collective-permute-done.12.refs_6_), channel_id=1, source_target_pairs={{0,7},{1,0},{2,1},{3,2},{4,3},{5,4},{6,5},{7,6},{8,15},{9,8},{10,9... | collective-permute-start | bytes 884744 | tf_op jit(solution)/shard_map/ppermute | solution.py:123
  74.9 0.0 collective-permute-done.9.refs_3_
  74.9 0.0 copy-start.11
  74.9 3.7 %collective-permute-start.10 = (bf16[8,144,128]{2,1,0:T(8,128)(2,1)S(1)}, bf16[8,144,128]{2,1,0:T(8,128)(2,1)}, u32[]{:S(2)}, u32[]{:S(2)}) collective-permute-start(bf16[8,144,128]{2,1,0:T(8,128)(2,1)S(1)} %collective-permute-done.9.refs_3_), channel_id=1, source_target_pairs={{0,1},{1,2},{2,3},{3,4},{4,5},{5,6},{6,7},{7,0},{8,9},{9,10},{10,1... | collective-permute-start | bytes 884744 | tf_op jit(solution)/shard_map/ppermute | solution.py:121
  78.7 0.0 collective-permute-done.1.refs_2_
  78.7 0.0 copy-start.8
  78.7 1.9 %collective-permute-start.2 = (bf16[8,144,128]{2,1,0:T(8,128)(2,1)S(1)}, bf16[8,144,128]{2,1,0:T(8,128)(2,1)}, u32[]{:S(2)}, u32[]{:S(2)}) collective-permute-start(bf16[8,144,128]{2,1,0:T(8,128)(2,1)S(1)} %collective-permute-done.1.refs_2_), channel_id=1, source_target_pairs={{0,1},{1,2},{2,3},{3,4},{4,5},{5,6},{6,7},{7,0},{8,9},{9,10},{10,1... | collective-permute-start | bytes 884744 | tf_op jit(solution)/shard_map/ppermute | solution.py:121
  80.6 0.0 collective-permute-done.5.refs_5_
  80.6 0.0 copy-start.10
  80.7 5.1 %collective-permute-start.6 = (bf16[8,144,128]{2,1,0:T(8,128)(2,1)S(1)}, bf16[8,144,128]{2,1,0:T(8,128)(2,1)}, u32[]{:S(2)}, u32[]{:S(2)}) collective-permute-start(bf16[8,144,128]{2,1,0:T(8,128)(2,1)S(1)} %collective-permute-done.5.refs_5_), channel_id=1, source_target_pairs={{0,7},{1,0},{2,1},{3,2},{4,3},{5,4},{6,5},{7,6},{8,15},{9,8},{10,9... | collective-permute-start | bytes 884744 | tf_op jit(solution)/shard_map/ppermute | solution.py:123
  85.8 1.8 %copy.9 = bf16[512,2,128]{0,2,1:T(8,128)(2,1)} copy(bf16[512,2,128]{2,1,0:T(2,128)(2,1)} %param.8) | data formatting | bytes 524288 | tf_op args[3]
  87.6 1.7 %copy.12 = bf16[64,8,2,128]{3,1,2,0:T(8,128)(2,1)} copy(bf16[64,8,2,128]{3,2,1,0:T(2,128)(2,1)} %bitcast.17) | data formatting | bytes 524288
  89.3 0.0 collective-permute-done.13.refs_5_
  89.3 0.0 collective-permute-done.10.refs_4_
  89.3 0.0 copy-done.1
  89.3 0.0 copy-done.3
  89.3 0.0 copy-done.6
  89.3 0.0 copy-done.7
  89.4 0.0 copy-done.9
  89.4 0.0 copy-done.11
  89.4 6.2 %expand.2 = (bf16[2,192,4096]{2,1,0:T(8,128)(2,1)}, bf16[8192,128]{1,0:T(8,128)(2,1)}) custom-call(s32[1]{0:T(128)} %bitcast.z_ref, bf16[256,512]{1,0:T(8,128)(2,1)} %bitcast.12, bf16[512,256]{1,0:T(8,128)(2,1)} %bitcast.14, bf16[8,144,128]{2,1,0:T(8,128)(2,1)} %copy-done.1, bf16[8,144,128]{2,1,0:T(8,128)(2,1)} %copy-done.3, bf16[8,144,128]{2,1,0:T(8,128)(2,1)} %copy-done.7, ...), custom_call_target="tpu_custom_call" | custom-call | tf_op jit(solution)/shard_map/expand/pallas_call | solution.py:95
  95.6 0.0 collective-permute-done.2.refs_3_
  95.6 0.0 collective-permute-done.6.refs_4_
  95.6 0.0 copy-done
  95.6 0.0 copy-done.2
  95.6 0.0 copy-done.4
  95.6 0.0 copy-done.5
  95.6 0.0 copy-done.8
  95.6 0.0 copy-done.10
  95.6 6.2 %expand.3 = (bf16[2,192,4096]{2,1,0:T(8,128)(2,1)}, bf16[8192,128]{1,0:T(8,128)(2,1)}) custom-call(s32[1]{0:T(128)} %bitcast.z_ref, bf16[256,512]{1,0:T(8,128)(2,1)} %bitcast.13, bf16[512,256]{1,0:T(8,128)(2,1)} %bitcast.15, bf16[8,144,128]{2,1,0:T(8,128)(2,1)} %copy-done, ...), custom_call_target="tpu_custom_call", output_to_operand_aliasing={{0}: (11, {}), {1}: (12, {})} | custom-call | tf_op jit(solution)/shard_map/expand/pallas_call | solution.py:95
  (1 shorter events, 0.0 us)
Async XLA Ops:
  29.0 60.4 %copy-start.1 = (bf16[8,144,128]{2,1,0:T(8,128)(2,1)}, bf16[8,144,128]{2,1,0:T(8,128)(2,1)S(1)}, u32[]{:S(2)}) copy-start(bf16[8,144,128]{2,1,0:T(8,128)(2,1)S(1)} %get-tuple-element.10.refs_0_) | copy-start | bytes 884740
  29.0 66.6 %copy-start = (bf16[8,144,128]{2,1,0:T(8,128)(2,1)}, bf16[8,144,128]{2,1,0:T(8,128)(2,1)S(1)}, u32[]{:S(2)}) copy-start(bf16[8,144,128]{2,1,0:T(8,128)(2,1)S(1)} %get-tuple-element.11.refs_0_) | copy-start | bytes 884740
  29.0 18.5 %collective-permute-start.7 = (bf16[8,144,128]{2,1,0:T(8,128)(2,1)S(1)}, bf16[8,144,128]{2,1,0:T(8,128)(2,1)S(1)}, u32[]{:S(2)}, u32[]{:S(2)}) collective-permute-start(bf16[8,144,128]{2,1,0:T(8,128)(2,1)S(1)} %get-tuple-element.10.refs_0_), channel_id=1, source_target_pairs={{0,1},{1,2},{2,3},{3,4},{4,5},{5,6},{6,7},{7,0},{8,9},{9,10},{10,1... | collective-permute-start | bytes 884744 | tf_op jit(solution)/shard_map/ppermute | solution.py:121
  33.3 18.1 %collective-permute-start.3 = (bf16[8,144,128]{2,1,0:T(8,128)(2,1)S(1)}, bf16[8,144,128]{2,1,0:T(8,128)(2,1)S(1)}, u32[]{:S(2)}, u32[]{:S(2)}) collective-permute-start(bf16[8,144,128]{2,1,0:T(8,128)(2,1)S(1)} %get-tuple-element.11.refs_0_), channel_id=1, source_target_pairs={{0,7},{1,0},{2,1},{3,2},{4,3},{5,4},{6,5},{7,6},{8,15},{9,8},{10,9... | collective-permute-start | bytes 884744 | tf_op jit(solution)/shard_map/ppermute | solution.py:123
  41.9 14.6 %collective-permute-start.11 = (bf16[8,144,128]{2,1,0:T(8,128)(2,1)S(1)}, bf16[8,144,128]{2,1,0:T(8,128)(2,1)S(1)}, u32[]{:S(2)}, u32[]{:S(2)}) collective-permute-start(bf16[8,144,128]{2,1,0:T(8,128)(2,1)S(1)} %get-tuple-element.10.refs_0_), channel_id=1, source_target_pairs={{0,7},{1,0},{2,1},{3,2},{4,3},{5,4},{6,5},{7,6},{8,15},{9,8},{10,9... | collective-permute-start | bytes 884744 | tf_op jit(solution)/shard_map/ppermute | solution.py:123
  47.5 41.8 %copy-start.3 = (bf16[8,144,128]{2,1,0:T(8,128)(2,1)}, bf16[8,144,128]{2,1,0:T(8,128)(2,1)S(1)}, u32[]{:S(2)}) copy-start(bf16[8,144,128]{2,1,0:T(8,128)(2,1)S(1)} %collective-permute-done.7.refs_1_) | copy-start | bytes 884740
  47.5 13.1 %collective-permute-start.8 = (bf16[8,144,128]{2,1,0:T(8,128)(2,1)S(1)}, bf16[8,144,128]{2,1,0:T(8,128)(2,1)S(1)}, u32[]{:S(2)}, u32[]{:S(2)}) collective-permute-start(bf16[8,144,128]{2,1,0:T(8,128)(2,1)S(1)} %collective-permute-done.7.refs_1_), channel_id=1, source_target_pairs={{0,1},{1,2},{2,3},{3,4},{4,5},{5,6},{6,7},{7,0},{8,9},{9,10},{10,1... | collective-permute-start | bytes 884744 | tf_op jit(solution)/shard_map/ppermute | solution.py:121
  49.4 16.3 %collective-permute-start = (bf16[8,144,128]{2,1,0:T(8,128)(2,1)S(1)}, bf16[8,144,128]{2,1,0:T(8,128)(2,1)S(1)}, u32[]{:S(2)}, u32[]{:S(2)}) collective-permute-start(bf16[8,144,128]{2,1,0:T(8,128)(2,1)S(1)} %get-tuple-element.11.refs_0_), channel_id=1, source_target_pairs={{0,1},{1,2},{2,3},{3,4},{4,5},{5,6},{6,7},{7,0},{8,9},{9,10},{10,1... | collective-permute-start | bytes 884744 | tf_op jit(solution)/shard_map/ppermute | solution.py:121
  51.3 44.2 %copy-start.2 = (bf16[8,144,128]{2,1,0:T(8,128)(2,1)}, bf16[8,144,128]{2,1,0:T(8,128)(2,1)S(1)}, u32[]{:S(2)}) copy-start(bf16[8,144,128]{2,1,0:T(8,128)(2,1)S(1)} %collective-permute-done.3.refs_7_) | copy-start | bytes 884740
  51.4 16.3 %collective-permute-start.4 = (bf16[8,144,128]{2,1,0:T(8,128)(2,1)S(1)}, bf16[8,144,128]{2,1,0:T(8,128)(2,1)S(1)}, u32[]{:S(2)}, u32[]{:S(2)}) collective-permute-start(bf16[8,144,128]{2,1,0:T(8,128)(2,1)S(1)} %collective-permute-done.3.refs_7_), channel_id=1, source_target_pairs={{0,7},{1,0},{2,1},{3,2},{4,3},{5,4},{6,5},{7,6},{8,15},{9,8},{10,9... | collective-permute-start | bytes 884744 | tf_op jit(solution)/shard_map/ppermute | solution.py:123
  56.5 32.8 %copy-start.6 = (bf16[8,144,128]{2,1,0:T(8,128)(2,1)}, bf16[8,144,128]{2,1,0:T(8,128)(2,1)S(1)}, u32[]{:S(2)}) copy-start(bf16[8,144,128]{2,1,0:T(8,128)(2,1)S(1)} %collective-permute-done.11.refs_7_) | copy-start | bytes 884740
  56.5 16.3 %collective-permute-start.12 = (bf16[8,144,128]{2,1,0:T(8,128)(2,1)S(1)}, bf16[8,144,128]{2,1,0:T(8,128)(2,1)S(1)}, u32[]{:S(2)}, u32[]{:S(2)}) collective-permute-start(bf16[8,144,128]{2,1,0:T(8,128)(2,1)S(1)} %collective-permute-done.11.refs_7_), channel_id=1, source_target_pairs={{0,7},{1,0},{2,1},{3,2},{4,3},{5,4},{6,5},{7,6},{8,15},{9,8},{10,9... | collective-permute-start | bytes 884744 | tf_op jit(solution)/shard_map/ppermute | solution.py:123
  60.6 28.7 %copy-start.7 = (bf16[8,144,128]{2,1,0:T(8,128)(2,1)}, bf16[8,144,128]{2,1,0:T(8,128)(2,1)S(1)}, u32[]{:S(2)}) copy-start(bf16[8,144,128]{2,1,0:T(8,128)(2,1)S(1)} %collective-permute-done.8.refs_2_) | copy-start | bytes 884740
  60.6 14.3 %collective-permute-start.9 = (bf16[8,144,128]{2,1,0:T(8,128)(2,1)S(1)}, bf16[8,144,128]{2,1,0:T(8,128)(2,1)S(1)}, u32[]{:S(2)}, u32[]{:S(2)}) collective-permute-start(bf16[8,144,128]{2,1,0:T(8,128)(2,1)S(1)} %collective-permute-done.8.refs_2_), channel_id=1, source_target_pairs={{0,1},{1,2},{2,3},{3,4},{4,5},{5,6},{6,7},{7,0},{8,9},{9,10},{10,1... | collective-permute-start | bytes 884744 | tf_op jit(solution)/shard_map/ppermute | solution.py:121
  65.7 29.9 %copy-start.4 = (bf16[8,144,128]{2,1,0:T(8,128)(2,1)}, bf16[8,144,128]{2,1,0:T(8,128)(2,1)S(1)}, u32[]{:S(2)}) copy-start(bf16[8,144,128]{2,1,0:T(8,128)(2,1)S(1)} %collective-permute-done.refs_1_) | copy-start | bytes 884740
  65.7 13.0 %collective-permute-start.1 = (bf16[8,144,128]{2,1,0:T(8,128)(2,1)S(1)}, bf16[8,144,128]{2,1,0:T(8,128)(2,1)S(1)}, u32[]{:S(2)}, u32[]{:S(2)}) collective-permute-start(bf16[8,144,128]{2,1,0:T(8,128)(2,1)S(1)} %collective-permute-done.refs_1_), channel_id=1, source_target_pairs={{0,1},{1,2},{2,3},{3,4},{4,5},{5,6},{6,7},{7,0},{8,9},{9,10},{10,1... | collective-permute-start | bytes 884744 | tf_op jit(solution)/shard_map/ppermute | solution.py:121
  67.6 28.0 %copy-start.5 = (bf16[8,144,128]{2,1,0:T(8,128)(2,1)}, bf16[8,144,128]{2,1,0:T(8,128)(2,1)S(1)}, u32[]{:S(2)}) copy-start(bf16[8,144,128]{2,1,0:T(8,128)(2,1)S(1)} %collective-permute-done.4.refs_6_) | copy-start | bytes 884740
  67.6 13.0 %collective-permute-start.5 = (bf16[8,144,128]{2,1,0:T(8,128)(2,1)S(1)}, bf16[8,144,128]{2,1,0:T(8,128)(2,1)S(1)}, u32[]{:S(2)}, u32[]{:S(2)}) collective-permute-start(bf16[8,144,128]{2,1,0:T(8,128)(2,1)S(1)} %collective-permute-done.4.refs_6_), channel_id=1, source_target_pairs={{0,7},{1,0},{2,1},{3,2},{4,3},{5,4},{6,5},{7,6},{8,15},{9,8},{10,9... | collective-permute-start | bytes 884744 | tf_op jit(solution)/shard_map/ppermute | solution.py:123
  72.8 16.6 %copy-start.9 = (bf16[8,144,128]{2,1,0:T(8,128)(2,1)}, bf16[8,144,128]{2,1,0:T(8,128)(2,1)S(1)}, u32[]{:S(2)}) copy-start(bf16[8,144,128]{2,1,0:T(8,128)(2,1)S(1)} %collective-permute-done.12.refs_6_) | copy-start | bytes 884740
  72.8 16.5 %collective-permute-start.13 = (bf16[8,144,128]{2,1,0:T(8,128)(2,1)S(1)}, bf16[8,144,128]{2,1,0:T(8,128)(2,1)}, u32[]{:S(2)}, u32[]{:S(2)}) collective-permute-start(bf16[8,144,128]{2,1,0:T(8,128)(2,1)S(1)} %collective-permute-done.12.refs_6_), channel_id=1, source_target_pairs={{0,7},{1,0},{2,1},{3,2},{4,3},{5,4},{6,5},{7,6},{8,15},{9,8},{10,9... | collective-permute-start | bytes 884744 | tf_op jit(solution)/shard_map/ppermute | solution.py:123
  74.9 14.4 %copy-start.11 = (bf16[8,144,128]{2,1,0:T(8,128)(2,1)}, bf16[8,144,128]{2,1,0:T(8,128)(2,1)S(1)}, u32[]{:S(2)}) copy-start(bf16[8,144,128]{2,1,0:T(8,128)(2,1)S(1)} %collective-permute-done.9.refs_3_) | copy-start | bytes 884740
  74.9 14.4 %collective-permute-start.10 = (bf16[8,144,128]{2,1,0:T(8,128)(2,1)S(1)}, bf16[8,144,128]{2,1,0:T(8,128)(2,1)}, u32[]{:S(2)}, u32[]{:S(2)}) collective-permute-start(bf16[8,144,128]{2,1,0:T(8,128)(2,1)S(1)} %collective-permute-done.9.refs_3_), channel_id=1, source_target_pairs={{0,1},{1,2},{2,3},{3,4},{4,5},{5,6},{6,7},{7,0},{8,9},{9,10},{10,1... | collective-permute-start | bytes 884744 | tf_op jit(solution)/shard_map/ppermute | solution.py:121
  78.7 16.9 %copy-start.8 = (bf16[8,144,128]{2,1,0:T(8,128)(2,1)}, bf16[8,144,128]{2,1,0:T(8,128)(2,1)S(1)}, u32[]{:S(2)}) copy-start(bf16[8,144,128]{2,1,0:T(8,128)(2,1)S(1)} %collective-permute-done.1.refs_2_) | copy-start | bytes 884740
  78.7 16.9 %collective-permute-start.2 = (bf16[8,144,128]{2,1,0:T(8,128)(2,1)S(1)}, bf16[8,144,128]{2,1,0:T(8,128)(2,1)}, u32[]{:S(2)}, u32[]{:S(2)}) collective-permute-start(bf16[8,144,128]{2,1,0:T(8,128)(2,1)S(1)} %collective-permute-done.1.refs_2_), channel_id=1, source_target_pairs={{0,1},{1,2},{2,3},{3,4},{4,5},{5,6},{6,7},{7,0},{8,9},{9,10},{10,1... | collective-permute-start | bytes 884744 | tf_op jit(solution)/shard_map/ppermute | solution.py:121
  80.6 15.0 %copy-start.10 = (bf16[8,144,128]{2,1,0:T(8,128)(2,1)}, bf16[8,144,128]{2,1,0:T(8,128)(2,1)S(1)}, u32[]{:S(2)}) copy-start(bf16[8,144,128]{2,1,0:T(8,128)(2,1)S(1)} %collective-permute-done.5.refs_5_) | copy-start | bytes 884740
  80.7 14.9 %collective-permute-start.6 = (bf16[8,144,128]{2,1,0:T(8,128)(2,1)S(1)}, bf16[8,144,128]{2,1,0:T(8,128)(2,1)}, u32[]{:S(2)}, u32[]{:S(2)}) collective-permute-start(bf16[8,144,128]{2,1,0:T(8,128)(2,1)S(1)} %collective-permute-done.5.refs_5_), channel_id=1, source_target_pairs={{0,7},{1,0},{2,1},{3,2},{4,3},{5,4},{6,5},{7,6},{8,15},{9,8},{10,9... | collective-permute-start | bytes 884744 | tf_op jit(solution)/shard_map/ppermute | solution.py:123
